TPU v7x, 32 devices: a whole 2x2x4 slice. The times are simulated.
32 devices in a mesh: gx: 4 (over z), gy: 4 (over y, core), af: 2 (over x).
Axes of the slice: x: 2, y: 2, z: 4, core: 2. Of those that a mesh axis runs over, the one named last changes fastest.
Arguments:
- points: bfloat16 [1024, 256], P(('gx', 'gy'), 'af'), may hold values from -12 to 12
- targets: float32 [1024, 16], P(('gx', 'gy')), may hold values from -6 to 6
Outputs:
- solution: float32 [1024, 16], P(('gx', 'gy'))
- residual: float32 [1024, 16], P(('gx', 'gy'))
All inputs are finite; a program needn't handle non-finite values.
Results may differ from a plain program's by a relative error of at most 0.025.
Values may be sent and summed in bfloat16 or wider, within the bound.
A program may use at most 64 MiB of HBM per device.

v0:
```python
import jax
import jax.numpy as jnp
from jax import lax
from jax.sharding import PartitionSpec as P

ITERS = 2


def point_norms(block):
    wide_block = block.astype(jnp.float32)
    return jnp.sum(wide_block * wide_block, axis=1)


def kernel_times(row_slab, slab_norms, col_slab, col_slab_norms, col_vector, scale):
    inner = lax.dot_general(
        row_slab, col_slab, (((1,), (1,)), ((), ())), preferred_element_type=jnp.float32
    )
    distance = slab_norms[:, None] + col_slab_norms[None, :] - 2.0 * inner
    kernel = jnp.exp(-scale * distance).astype(jnp.bfloat16)
    return jnp.dot(kernel, col_vector, preferred_element_type=jnp.float32)


def split_size(count):
    block_size = count
    while block_size > 1024 and block_size % 2 == 0:
        block_size = block_size // 2
    return block_size


def local(points, targets):
    whole_feat = lax.all_gather(points, "af", axis=1, tiled=True)
    norms = point_norms(whole_feat)
    half_rows = whole_feat.shape[0] // 2
    start_row = lax.axis_index("af") * half_rows
    my_points = lax.dynamic_slice_in_dim(whole_feat, start_row, half_rows, 0)
    scale = 0.5 / whole_feat.shape[1]
    stored_points = lax.all_gather(my_points, ("gx", "gy"), axis=0, tiled=True)
    stored_norms = point_norms(stored_points)

    def operate(vector):
        lowered = vector.astype(jnp.bfloat16)
        my_vector = lax.dynamic_slice_in_dim(lowered, start_row, half_rows, 0)
        empty = jnp.zeros(vector.shape, jnp.float32)
        piece = lax.all_gather(my_vector, ("gx", "gy"), axis=0, tiled=True)
        count = piece.shape[0]
        block_size = split_size(count)

        def one_block(carry, index):
            offset = index * block_size
            col_slab = lax.dynamic_slice_in_dim(stored_points, offset, block_size, 0)
            col_slab_norms = lax.dynamic_slice_in_dim(stored_norms, offset, block_size, 0)
            vector_slab = lax.dynamic_slice_in_dim(piece, offset, block_size, 0)
            return (
                carry
                + kernel_times(whole_feat, norms, col_slab, col_slab_norms, vector_slab, scale),
                None,
            )

        result, unused = lax.scan(
            one_block, empty, jnp.arange(count // block_size, dtype=jnp.int32)
        )
        return lax.psum(result, "af") + 0.1 * vector

    def two_products(values, image):
        return lax.psum(
            (jnp.sum(values * values, axis=0), jnp.sum(values * image, axis=0)), ("gx", "gy")
        )

    solution = jnp.zeros_like(targets)
    residual = targets
    image = operate(residual)
    norm_now, product = two_products(residual, image)
    alpha = norm_now / product
    direction = residual
    along = image
    for step in range(ITERS):
        solution = solution + alpha * direction
        residual = residual - alpha * along
        if step + 1 < ITERS:
            image = operate(residual)
            norm_next, product = two_products(residual, image)
            ratio = norm_next / norm_now
            alpha = norm_next / (product - ratio * norm_next / alpha)
            direction = residual + ratio * direction
            along = image + ratio * along
            norm_now = norm_next
    return (solution, residual)


def solution(mesh):
    placed = (P(("gx", "gy"), "af"), P(("gx", "gy"), None))
    return jax.shard_map(
        local,
        mesh=mesh,
        in_specs=placed,
        out_specs=(P(("gx", "gy"), None), P(("gx", "gy"), None)),
        check_vma=False,
    )
```

profile of v0, /device:TPU:1, one launch (start us, length us, event | category | flops | bytes accessed | tf_op | source)
XLA Modules:
  0.0 135.4 jit_solution(6535780304022626250)
XLA Ops:
  0.6 4.1 %all_gather.12 = bf16[64,256]{1,0:T(8,128)(2,1)S(1)} all-gather(bf16[64,128]{1,0:T(8,128)(2,1)} %param.2), channel_id=1, replica_groups=mesh['gx'=4,'gy'=4,'af'=2] {'af'}, dimensions={1}, use_global_device_ids=true | all-gather | bytes 49152 | tf_op jit(solution)/shard_map/all_gather | solution.py:31
  4.8 24.2 %all_gather.13 = bf16[512,256]{1,0:T(8,128)(2,1)S(1)} all-gather(bf16[32,256]{1,0:T(8,128)(2,1)S(1)} %constant_dynamic-slice_fusion), channel_id=1, replica_groups=mesh['gx'=4,'gy'=4,'af'=2] {'gx','gy'}, dimensions={0}, use_global_device_ids=true | all-gather | bytes 278528 | tf_op jit(solution)/shard_map/all_gather | solution.py:37
  29.0 0.1 multiply_reduce_fusion
  29.1 0.1 multiply_reduce_fusion.1
  29.2 0.0 copy-start
  29.2 0.2 fusion.4
  29.5 0.5 copy-done
  29.9 0.1 fusion.5
  30.0 17.6 %all-gather = bf16[16,32,16]{1,2,0:T(8,128)(2,1)S(1)} all-gather(bf16[1,32,16]{1,2,0:T(8,128)(2,1)S(1)} %fusion.5), channel_id=1, replica_groups=mesh['gx'=4,'gy'=4,'af'=2] {'gx','gy'}, dimensions={0}, use_global_device_ids=true | all-gather | bytes 17408 | tf_op jit(solution)/shard_map/all_gather | solution.py:44
  47.6 0.1 reshape.10
  47.7 0.1 fusion.7
  47.8 3.8 %psum.43 = f32[64,16]{0,1:T(8,128)S(1)} all-reduce(f32[64,16]{0,1:T(8,128)S(1)} %fusion.7), channel_id=1, replica_groups=mesh['gx'=4,'gy'=4,'af'=2] {'af'}, use_global_device_ids=true, to_apply=%region_4.5 | all-reduce | flops 1024 | bytes 8192 | tf_op jit(solution)/shard_map/psum | solution.py:62
  51.7 0.1 multiply_reduce_fusion.4
  51.8 30.2 %all-reduce.1 = (f32[16]{0:T(128)S(1)}, f32[16]{0:T(128)S(1)}) all-reduce(f32[16]{0:T(128)S(1)} %get-tuple-element.33, f32[16]{0:T(128)S(1)} %get-tuple-element.32), channel_id=1, replica_groups=mesh['gx'=4,'gy'=4,'af'=2] {'gx','gy'}, use_global_device_ids=true, to_apply=%region_1.0 | all-reduce | flops 32 | bytes 256 | tf_op jit(solution)/shard_map/psum | solution.py:65
  82.0 0.1 multiply_subtract_fusion.1
  82.0 0.1 fusion.6
  82.1 18.2 %all-gather.1 = bf16[16,32,16]{1,2,0:T(8,128)(2,1)S(1)} all-gather(bf16[1,32,16]{1,2,0:T(8,128)(2,1)S(1)} %fusion.6), channel_id=1, replica_groups=mesh['gx'=4,'gy'=4,'af'=2] {'gx','gy'}, dimensions={0}, use_global_device_ids=true | all-gather | bytes 17408 | tf_op jit(solution)/shard_map/all_gather | solution.py:44
  100.4 0.1 reshape.12
  100.5 0.1 fusion.8
  100.6 3.8 %psum.46 = f32[64,16]{0,1:T(8,128)S(1)} all-reduce(f32[64,16]{0,1:T(8,128)S(1)} %fusion.8), channel_id=1, replica_groups=mesh['gx'=4,'gy'=4,'af'=2] {'af'}, use_global_device_ids=true, to_apply=%region_9.10 | all-reduce | flops 1024 | bytes 8192 | tf_op jit(solution)/shard_map/psum | solution.py:62
  104.4 0.1 multiply_reduce_fusion.2
  104.5 30.2 %all-reduce = (f32[16]{0:T(128)S(1)}, f32[16]{0:T(128)S(1)}) all-reduce(f32[16]{0:T(128)S(1)} %get-tuple-element.31, f32[16]{0:T(128)S(1)} %get-tuple-element.30), channel_id=1, replica_groups=mesh['gx'=4,'gy'=4,'af'=2] {'gx','gy'}, use_global_device_ids=true, to_apply=%region_8.9 | all-reduce | flops 32 | bytes 256 | tf_op jit(solution)/shard_map/psum | solution.py:65
  134.7 0.7 multiply_subtract_fusion
  (5 shorter events, 0.1 us)
Async XLA Ops:
  29.2 0.7 copy-start
where the time goes:
time: 137 us; the launch traced here: 135 us
  blocking collectives  132 us (96%)
    psum x2, blocking collectives, two_products(): lax.psum((jnp.sum(values * values, axis=0), jnp.sum(values * image, axis=...  60.3 us
    all_gather x2, blocking collectives, operate(): piece = lax.all_gather(my_vector, ('gx', 'gy'), axis=0, tiled=True)  35.8 us
    all_gather x1, blocking collectives, local(): stored_points = lax.all_gather(my_points, ('gx', 'gy'), axis=0, tiled=True)  24.2 us
    psum x2, blocking collectives, operate(): return lax.psum(result, 'af') + 0.1 * vector  7.63 us
    all_gather x1, blocking collectives, local(): whole_feat = lax.all_gather(points, 'af', axis=1, tiled=True)  4.12 us

commit v1 on v0

--- a/solution.py
+++ b/solution.py
@@ -1,9 +1,17 @@
+import functools
+import math
+
 import jax
 import jax.numpy as jnp
 from jax import lax
+from jax.experimental import pallas as pl
+from jax.experimental.pallas import tpu as pltpu
 from jax.sharding import PartitionSpec as P
 
 ITERS = 2
+MESH = pl.DeviceIdType.MESH
+LANES = 128
+CORES = 2
 
 
 def point_norms(block):
@@ -27,10 +35,10 @@
     return block_size
 
 
-def local(points, targets):
+def local_large(points, targets):
     whole_feat = lax.all_gather(points, "af", axis=1, tiled=True)
     norms = point_norms(whole_feat)
-    half_rows = whole_feat.shape[0] // 2
+    half_rows = whole_feat.shape[0] // lax.axis_size("af")
     start_row = lax.axis_index("af") * half_rows
     my_points = lax.dynamic_slice_in_dim(whole_feat, start_row, half_rows, 0)
     scale = 0.5 / whole_feat.shape[1]
@@ -87,12 +95,223 @@
     return (solution, residual)
 
 
+def gather_and_solve(
+    sizes, pts_hbm, tgt_hbm, sol_ref, res_ref, pts, tgt, kmat, stage,
+    local_sem, psend, precv, tsend, trecv,
+):
+    nz, nw, nx = sizes
+    ny = nw // CORES
+    count, feats = pts_hbm.shape
+    rhs = tgt_hbm.shape[0]
+    z, w, x = lax.axis_index("gx"), lax.axis_index("gy"), lax.axis_index("af")
+    y, c = w // CORES, w % CORES
+    other = y * CORES + (1 - c)
+
+    def shift(value, by, size):
+        return lax.rem(value + by, size)
+
+    sends = []
+
+    def points_at(zb, wb, xb):
+        rows = pl.ds(pl.multiple_of((zb * nw + wb) * count, count), count)
+        return pts.at[rows, pl.ds(pl.multiple_of(xb * feats, feats), feats)]
+
+    def points_copy(block, to, slot):
+        zb, wb, xb = block
+        where = points_at(zb, wb, xb)
+        return pltpu.make_async_remote_copy(
+            src_ref=where, dst_ref=where, send_sem=psend.at[slot],
+            recv_sem=precv.at[xb, zb * nw + wb], device_id=to, device_id_type=MESH,
+        )
+
+    def targets_copy(block, to, slot):
+        zb, wb = block
+        where = tgt.at[zb * nw + wb]
+        return pltpu.make_async_remote_copy(
+            src_ref=where, dst_ref=where, send_sem=tsend.at[slot],
+            recv_sem=trecv.at[zb * nw + wb], device_id=to, device_id_type=MESH,
+        )
+
+    used = {"p": 0, "t": 0}
+
+    def send(kind, block, to):
+        make = points_copy if kind == "p" else targets_copy
+        copy = make(block, to, used[kind])
+        used[kind] += 1
+        copy.start()
+        sends.append(copy)
+
+    def arrived(kind, block):
+        make = points_copy if kind == "p" else targets_copy
+        make(block, (z, other, x), 0).wait_recv()
+
+    line = [(shift(z, d, nz), w, x) for d in range(1, nz)]
+    plane = [
+        (dy, dx, (z, shift(y, dy, ny) * CORES + c, shift(x, dx, nx)))
+        for dy in range(ny) for dx in range(nx) if dy or dx
+    ]
+    partner = (z, other, x)
+
+    own_points = pltpu.make_async_copy(pts_hbm, points_at(z, w, x), local_sem.at[0])
+    own_targets = pltpu.make_async_copy(tgt_hbm, tgt.at[z * nw + w], local_sem.at[1])
+    own_points.start()
+    own_targets.start()
+    barrier = pltpu.get_barrier_semaphore()
+    peers = line + [to for dy, dx, to in plane] + [partner]
+    for to in peers:
+        pl.semaphore_signal(barrier, inc=1, device_id=to, device_id_type=MESH)
+    own_points.wait()
+    own_targets.wait()
+    pl.semaphore_wait(barrier, len(peers))
+
+    def to_plane(zb):
+        for dy, dx, to in plane:
+            send("p", (zb, w, x), to)
+            if dx == 0:
+                send("t", (zb, w), to)
+        send("p", (zb, w, x), partner)
+        send("t", (zb, w), partner)
+
+    for to in line:
+        send("p", (z, w, x), to)
+        send("t", (z, w), to)
+    to_plane(z)
+    for d in range(1, nz):
+        zb = shift(z, d, nz)
+        arrived("p", (zb, w, x))
+        arrived("t", (zb, w))
+        to_plane(zb)
+    for d in range(nz):
+        zb = shift(z, d, nz)
+        for dy, dx, to in plane:
+            arrived("p", (zb, to[1], to[2]))
+            send("p", (zb, to[1], to[2]), partner)
+            if dx == 0:
+                arrived("t", (zb, to[1]))
+                send("t", (zb, to[1]), partner)
+    for d in range(nz):
+        zb = shift(z, d, nz)
+        for dy in range(ny):
+            wb = shift(y, dy, ny) * CORES + (1 - c)
+            for dx in range(nx):
+                arrived("p", (zb, wb, shift(x, dx, nx)))
+            arrived("t", (zb, wb))
+
+    total, width = pts.shape
+    factor = math.log2(math.e) / (2.0 * width)
+    wide = pts[...].astype(jnp.float32)
+    square = wide * wide
+    high = square.astype(jnp.bfloat16)
+    low = (square - high.astype(jnp.float32)).astype(jnp.bfloat16)
+    ones_col = jnp.ones((width, LANES), jnp.bfloat16)
+    ones_row = jnp.ones((16, width), jnp.bfloat16)
+    by_row = (((1,), (1,)), ((), ()))
+    norm_col = factor * (
+        jnp.dot(high, ones_col, preferred_element_type=jnp.float32)
+        + jnp.dot(low, ones_col, preferred_element_type=jnp.float32)
+    )
+    norm_row = factor * (
+        lax.dot_general(ones_row, high, by_row, preferred_element_type=jnp.float32)
+        + lax.dot_general(ones_row, low, by_row, preferred_element_type=jnp.float32)
+    )
+    block = 256
+    for j in range(total // block):
+        cols = slice(j * block, (j + 1) * block)
+        inner = lax.dot_general(
+            pts[...], pts[cols, :], by_row, preferred_element_type=jnp.float32
+        )
+        for k in range(block // LANES):
+            at = slice(j * block + k * LANES, j * block + (k + 1) * LANES)
+            power = (2.0 * factor) * inner[:, k * LANES:(k + 1) * LANES] - (
+                norm_col + norm_row[0:1, at]
+            )
+            kmat[:, at] = jnp.exp2(power).astype(jnp.bfloat16)
+
+    def operate(vector):
+        return jnp.dot(
+            vector.astype(jnp.bfloat16), kmat[...], preferred_element_type=jnp.float32
+        ) + 0.1 * vector
+
+    def over_points(values):
+        return jnp.sum(values, axis=1, keepdims=True)
+
+    residual = jnp.concatenate([tgt[g] for g in range(nz * nw)], axis=1)
+    direction = residual
+    solution = jnp.zeros_like(residual)
+    norm_now = over_points(residual * residual)
+    for step in range(ITERS):
+        image = operate(direction)
+        alpha = norm_now / over_points(direction * image)
+        solution = solution + alpha * direction
+        residual = residual - alpha * image
+        if step + 1 < ITERS:
+            norm_next = over_points(residual * residual)
+            direction = residual + (norm_next / norm_now) * direction
+            norm_now = norm_next
+    own = z * nw + w
+    per = LANES // count
+    for index, (values, out) in enumerate(((solution, sol_ref), (residual, res_ref))):
+        for k in range(total // LANES):
+            stage[index, k] = values[:, k * LANES:(k + 1) * LANES]
+        piece = stage[index, own // per]
+        mine = piece[:, 0:count]
+        for k in range(1, per):
+            mine = jnp.where(own % per == k, piece[:, k * count:(k + 1) * count], mine)
+        out[...] = mine
+    for copy in sends:
+        copy.wait_send()
+
+
+def local_small(sizes, points, targets):
+    nz, nw, nx = sizes
+    count, feats = points.shape
+    rhs = targets.shape[1]
+    total, width = nz * nw * count, nx * feats
+    groups = nz * nw
+    ny = nw // CORES
+    point_sends = (nz - 1) + nz * (ny * nx) + nz * (ny * nx - 1)
+    target_sends = (nz - 1) + nz * ny + nz * (ny - 1)
+    out = jax.ShapeDtypeStruct((rhs, count), jnp.float32)
+    sol, res = pl.pallas_call(
+        functools.partial(gather_and_solve, sizes),
+        out_shape=(out, out),
+        in_specs=[pl.BlockSpec(memory_space=pl.ANY)] * 2,
+        out_specs=[pl.BlockSpec(memory_space=pltpu.VMEM)] * 2,
+        scratch_shapes=[
+            pltpu.VMEM((total, width), jnp.bfloat16),
+            pltpu.VMEM((groups, rhs, count), jnp.float32),
+            pltpu.VMEM((total, total), jnp.bfloat16),
+            pltpu.VMEM((2, total // LANES, rhs, LANES), jnp.float32),
+            pltpu.SemaphoreType.DMA((2,)),
+            pltpu.SemaphoreType.DMA((point_sends,)),
+            pltpu.SemaphoreType.DMA((nx, groups)),
+            pltpu.SemaphoreType.DMA((target_sends,)),
+            pltpu.SemaphoreType.DMA((groups,)),
+        ],
+        compiler_params=pltpu.CompilerParams(collective_id=0, has_side_effects=True),
+    )(points, targets.T)
+    return sol.T, res.T
+
+
 def solution(mesh):
-    placed = (P(("gx", "gy"), "af"), P(("gx", "gy"), None))
+    sizes = tuple(mesh.shape[name] for name in ("gx", "gy", "af"))
+
+    def local(points, targets):
+        groups = sizes[0] * sizes[1]
+        total = groups * points.shape[0]
+        fits = 12 * total * total <= 32 * 2**20
+        aligned = (
+            sizes[1] % CORES == 0 and LANES % points.shape[0] == 0
+            and points.shape[1] % LANES == 0 and total % 256 == 0
+        )
+        if fits and aligned:
+            return local_small(sizes, points, targets)
+        return local_large(points, targets)
+
     return jax.shard_map(
         local,
         mesh=mesh,
-        in_specs=placed,
+        in_specs=(P(("gx", "gy"), "af"), P(("gx", "gy"), None)),
         out_specs=(P(("gx", "gy"), None), P(("gx", "gy"), None)),
         check_vma=False,
     )

time: 137 us -> 20.6 us (0.15)
  blocking collectives: 132 us -> 0 us
  Pallas kernels: 0 us -> 17.8 us
    psum x4 -> x0, blocking collectives: 68 us -> none  [the longest x2 60.3 us: two_products(): lax.psum((jnp.sum(values * values, axis=0), jnp.sum(values * image, axis=...]
    all_gather x4 -> x0, blocking collectives: 64.1 us -> none  [the longest x2 35.8 us: operate(): piece = lax.all_gather(my_vector, ('gx', 'gy'), axis=0, tiled=True)]
    pallas_call x0 -> x1, Pallas kernels: none -> 17.8 us  [local_small(): pl.pallas_call(functools.partial(gather_and_solve, sizes), out_shape=(out...]
where the time goes in v1:
time: 20.6 us; the launch traced here: 20.4 us
  Pallas kernels  17.8 us (86%)
  local copies, waits for them, and re-layouts  1.9 us (9%)
  between operations  0.65 us (3%)
    pallas_call x1, Pallas kernels, local_small(): pl.pallas_call(functools.partial(gather_and_solve, sizes), out_shape=(out...  17.8 us
    unnamed x4, local copies, waits for them, and re-layouts  1.9 us

profile of v1, /device:TPU:1, one launch (start us, length us, event | category | flops | bytes accessed | tf_op | source)
XLA Modules:
  0.0 20.4 jit_solution(9171171619457348616)
XLA Ops:
  0.6 17.8 %shard_map.41 = (f32[16,64]{1,0:T(8,128)}, f32[16,64]{1,0:T(8,128)}) custom-call(bf16[64,128]{1,0:T(8,128)(2,1)} %pts_hbm.1, f32[16,64]{1,0:T(8,128)} %bitcast.3), custom_call_target="tpu_custom_call" | custom-call | tf_op jit(solution)/shard_map/pallas_call | solution.py:275
  18.4 0.0 copy-start
  18.5 1.3 %copy.6 = f32[64,16]{0,1:T(8,128)} copy(f32[64,16]{0,1:T(8,128)} %bitcast.5) | data formatting | bytes 8192
  19.8 0.0 copy-done
  19.8 0.6 %copy.7 = f32[64,16]{0,1:T(8,128)} copy(f32[64,16]{0,1:T(8,128)S(1)} %bitcast.4) | data formatting | bytes 8192
Async XLA Ops:
  18.4 1.3 %copy-start = (f32[16,64]{1,0:T(8,128)S(1)}, f32[16,64]{1,0:T(8,128)}, u32[]{:S(2)}) copy-start(f32[16,64]{1,0:T(8,128)} %get-tuple-element.5) | copy-start | bytes 12292

commit v2 on v0

--- a/solution.py
+++ b/solution.py
@@ -1,9 +1,17 @@
+import functools
+import math
+
 import jax
 import jax.numpy as jnp
 from jax import lax
+from jax.experimental import pallas as pl
+from jax.experimental.pallas import tpu as pltpu
 from jax.sharding import PartitionSpec as P
 
 ITERS = 2
+MESH = pl.DeviceIdType.MESH
+LANES = 128
+CORES = 2
 
 
 def point_norms(block):
@@ -27,10 +35,10 @@
     return block_size
 
 
-def local(points, targets):
+def local_large(points, targets):
     whole_feat = lax.all_gather(points, "af", axis=1, tiled=True)
     norms = point_norms(whole_feat)
-    half_rows = whole_feat.shape[0] // 2
+    half_rows = whole_feat.shape[0] // lax.axis_size("af")
     start_row = lax.axis_index("af") * half_rows
     my_points = lax.dynamic_slice_in_dim(whole_feat, start_row, half_rows, 0)
     scale = 0.5 / whole_feat.shape[1]
@@ -87,12 +95,234 @@
     return (solution, residual)
 
 
+def gather_and_solve(
+    sizes, pts_hbm, tgt_hbm, base_ref, along_ref, alpha_ref, pts, tgt, kmat, norm_cols, norm_rows,
+    local_sem, psend, precv, tsend, trecv,
+):
+    nz, nw, nx = sizes
+    ny = nw // CORES
+    count, feats = pts_hbm.shape
+    z, w, x = lax.axis_index("gx"), lax.axis_index("gy"), lax.axis_index("af")
+    y, c = w // CORES, w % CORES
+    partner = (z, y * CORES + (1 - c), x)
+
+    def points_at(d, wb, xb):
+        rows = pl.ds(pl.multiple_of((d * nw + wb) * count, count), count)
+        return pts.at[rows, pl.ds(pl.multiple_of(xb * feats, feats), feats)]
+
+    def make(kind, block, to, slot, lands):
+        d, wb, xb = block
+        if kind == "p":
+            return pltpu.make_async_remote_copy(
+                src_ref=points_at(d, wb, xb), dst_ref=points_at(lands, wb, xb),
+                send_sem=psend.at[slot], recv_sem=precv.at[lands, wb, xb],
+                device_id=to, device_id_type=MESH,
+            )
+        return pltpu.make_async_remote_copy(
+            src_ref=tgt.at[d * nw + wb], dst_ref=tgt.at[lands * nw + wb],
+            send_sem=tsend.at[slot], recv_sem=trecv.at[lands, wb],
+            device_id=to, device_id_type=MESH,
+        )
+
+    def arrived(kind, block):
+        make(kind, block, partner, 0, block[0]).wait_recv()
+
+    sends = []
+    used = {"p": 0, "t": 0}
+
+    def send(kind, block, to, lands):
+        slot = used[kind]
+        used[kind] += 1
+        copy = make(kind, block, to, slot, lands)
+        copy.start()
+        sends.append(copy)
+
+    line = [(d, (lax.rem(z + d, nz), w, x)) for d in range(1, nz)]
+    plane = []
+    for dy in range(ny):
+        for dx in range(nx):
+            if dy or dx:
+                yb, xb = lax.rem(y + dy, ny), lax.rem(x + dx, nx)
+                plane.append((dx, yb * CORES + c, xb))
+
+    own_points = pltpu.make_async_copy(pts_hbm, points_at(0, w, x), local_sem.at[0])
+    own_targets = pltpu.make_async_copy(tgt_hbm, tgt.at[w], local_sem.at[1])
+    own_points.start()
+    own_targets.start()
+    barrier = pltpu.get_barrier_semaphore()
+    peers = [to for d, to in line] + [(z, wb, xb) for dx, wb, xb in plane] + [partner]
+    for to in peers:
+        pl.semaphore_signal(barrier, inc=1, device_id=to, device_id_type=MESH)
+    own_points.wait()
+    own_targets.wait()
+    pl.semaphore_wait(barrier, len(peers))
+
+    def to_chip_plane(d):
+        for dx, wb, xb in plane:
+            send("p", (d, w, x), (z, wb, xb), d)
+            if dx == 0:
+                send("t", (d, w, x), (z, wb, xb), d)
+        send("p", (d, w, x), partner, d)
+        send("t", (d, w, x), partner, d)
+
+    for d, to in line:
+        send("p", (0, w, x), to, nz - d)
+        send("t", (0, w, x), to, nz - d)
+    to_chip_plane(0)
+    for d in range(1, nz):
+        arrived("p", (d, w, x))
+        arrived("t", (d, w, x))
+        to_chip_plane(d)
+
+    def spread(d):
+        for dx, wb, xb in plane:
+            arrived("p", (d, wb, xb))
+            send("p", (d, wb, xb), partner, d)
+            if dx == 0:
+                arrived("t", (d, wb, xb))
+                send("t", (d, wb, xb), partner, d)
+
+    def collect(d):
+        for dy in range(ny):
+            wb = lax.rem(y + dy, ny) * CORES + (1 - c)
+            for dx in range(nx):
+                arrived("p", (d, wb, lax.rem(x + dx, nx)))
+            arrived("t", (d, wb, x))
+
+    total, width = pts.shape
+    group = total // nz
+    factor = math.log2(math.e) / (2.0 * width)
+    by_row = (((1,), (1,)), ((), ()))
+
+    def make_norms(rows):
+        wide = pts[rows, :].astype(jnp.float32)
+        square = wide * wide
+        high = square.astype(jnp.bfloat16)
+        low = (square - high.astype(jnp.float32)).astype(jnp.bfloat16)
+        ones_col = jnp.ones((width, LANES), jnp.bfloat16)
+        ones_row = jnp.ones((16, width), jnp.bfloat16)
+        norm_cols[rows, :] = factor * (
+            jnp.dot(high, ones_col, preferred_element_type=jnp.float32)
+            + jnp.dot(low, ones_col, preferred_element_type=jnp.float32)
+        )
+        norm_rows[:, rows] = factor * (
+            lax.dot_general(ones_row, high, by_row, preferred_element_type=jnp.float32)
+            + lax.dot_general(ones_row, low, by_row, preferred_element_type=jnp.float32)
+        )
+
+    def make_kernel(rows, cols):
+        inner = lax.dot_general(
+            pts[rows, :], pts[cols, :], by_row, preferred_element_type=jnp.float32
+        )
+        for k in range((cols.stop - cols.start) // LANES):
+            at = slice(cols.start + k * LANES, cols.start + (k + 1) * LANES)
+            power = (2.0 * factor) * inner[:, k * LANES:(k + 1) * LANES] - (
+                norm_cols[rows, :] + norm_rows[0:1, at]
+            )
+            kmat[rows, at] = jnp.exp2(power).astype(jnp.bfloat16)
+
+    for d in range(nz):
+        spread(d)
+    for d in range(nz):
+        collect(d)
+        new = slice(d * group, (d + 1) * group)
+        make_norms(new)
+        make_kernel(slice(0, (d + 1) * group), new)
+        for e in range(d):
+            make_kernel(new, slice(e * group, (e + 1) * group))
+
+    def operate(vector):
+        return jnp.dot(
+            vector.astype(jnp.bfloat16), kmat[...], preferred_element_type=jnp.float32
+        ) + 0.1 * vector
+
+    def over_points(values):
+        return jnp.sum(values, axis=1, keepdims=True)
+
+    def mine(values):
+        piece = values[:, 0:count]
+        for k in range(1, nw):
+            piece = jnp.where(w == k, values[:, k * count:(k + 1) * count], piece)
+        return piece
+
+    residual = jnp.concatenate([tgt[g] for g in range(nz * nw)], axis=1)
+    direction = residual
+    solution = jnp.zeros_like(residual)
+    norm_now = over_points(residual * residual)
+    for step in range(ITERS):
+        image = operate(direction)
+        alpha = norm_now / over_points(direction * image)
+        if step + 1 < ITERS:
+            solution = solution + alpha * direction
+            residual = residual - alpha * image
+            norm_next = over_points(residual * residual)
+            direction = residual + (norm_next / norm_now) * direction
+            norm_now = norm_next
+    base_ref[0] = mine(solution)
+    base_ref[1] = mine(residual)
+    along_ref[0] = mine(direction)
+    along_ref[1] = mine(image)
+    alpha_ref[...] = jnp.broadcast_to(alpha, alpha_ref.shape)
+
+    for copy in sends:
+        copy.wait_send()
+
+
+def local_small(sizes, points, targets):
+    nz, nw, nx = sizes
+    count, feats = points.shape
+    rhs = targets.shape[1]
+    total, width = nz * nw * count, nx * feats
+    groups = nz * nw
+    ny = nw // CORES
+    most_sends = 2 * nz * nw * nx + CORES * nz * ny * nx
+    base, along, alpha = pl.pallas_call(
+        functools.partial(gather_and_solve, sizes),
+        out_shape=(
+            pltpu.VMEM((2, rhs, count), jnp.float32),
+            pltpu.VMEM((2, rhs, count), jnp.float32),
+            pltpu.VMEM((rhs, count), jnp.float32),
+        ),
+        in_specs=[pl.BlockSpec(memory_space=pl.ANY)] * 2,
+        out_specs=[pl.BlockSpec(memory_space=pltpu.VMEM)] * 3,
+        scratch_shapes=[
+            pltpu.VMEM((total, width), jnp.bfloat16),
+            pltpu.VMEM((groups, rhs, count), jnp.float32),
+            pltpu.VMEM((total, total), jnp.bfloat16),
+            pltpu.VMEM((total, LANES), jnp.float32),
+            pltpu.VMEM((16, total), jnp.float32),
+            pltpu.SemaphoreType.DMA((2,)),
+            pltpu.SemaphoreType.DMA((most_sends,)),
+            pltpu.SemaphoreType.DMA((nz, nw, nx)),
+            pltpu.SemaphoreType.DMA((most_sends,)),
+            pltpu.SemaphoreType.DMA((nz, nw)),
+        ],
+        compiler_params=pltpu.CompilerParams(collective_id=0, has_side_effects=True),
+    )(points, targets.T)
+    last = base[0] + alpha * along[0]
+    left = base[1] - alpha * along[1]
+    return last.T, left.T
+
+
 def solution(mesh):
-    placed = (P(("gx", "gy"), "af"), P(("gx", "gy"), None))
+    sizes = tuple(mesh.shape[name] for name in ("gx", "gy", "af"))
+
+    def local(points, targets):
+        groups = sizes[0] * sizes[1]
+        total = groups * points.shape[0]
+        fits = 12 * total * total <= 32 * 2**20
+        aligned = (
+            sizes[1] % CORES == 0 and LANES % points.shape[0] == 0
+            and points.shape[1] % LANES == 0 and total % 256 == 0
+        )
+        if fits and aligned:
+            return local_small(sizes, points, targets)
+        return local_large(points, targets)
+
     return jax.shard_map(
         local,
         mesh=mesh,
-        in_specs=placed,
+        in_specs=(P(("gx", "gy"), "af"), P(("gx", "gy"), None)),
         out_specs=(P(("gx", "gy"), None), P(("gx", "gy"), None)),
         check_vma=False,
     )

time: 137 us -> 19.7 us (0.14)
  the two profiles are of different devices: /device:TPU:1 before, /device:TPU:0 now
where the time goes in v2:
time: 19.7 us; the launch traced here: 19.5 us
  Pallas kernels  18.3 us (93%)
  between operations  0.64 us (3%)
  other arithmetic  0.61 us (3%)
    pallas_call x1, Pallas kernels, local_small(): pl.pallas_call(functools.partial(gather_and_solve, sizes), out_shape=(plt...  18.3 us
    transpose x1, other arithmetic, local_small(): return (last.T, left.T)  0.61 us

profile of v2, /device:TPU:0, one launch (start us, length us, event | category | flops | bytes accessed | tf_op | source)
XLA Modules:
  0.0 19.5 jit_solution(9005744544046316346)
XLA Ops:
  0.6 18.3 %shard_map.41 = (f32[2,16,64]{2,1,0:T(8,128)S(1)}, f32[2,16,64]{2,1,0:T(8,128)S(1)}, f32[16,64]{1,0:T(8,128)S(1)}) custom-call(bf16[64,128]{1,0:T(8,128)(2,1)} %pts_hbm.1, f32[16,64]{1,0:T(8,128)} %bitcast.21), custom_call_target="tpu_custom_call" | custom-call | tf_op jit(solution)/shard_map/pallas_call | solution.py:279
  18.9 0.6 %fusion.1 = (f32[64,16]{0,1:T(8,128)}, f32[64,16]{0,1:T(8,128)}) fusion(f32[16,64]{1,0:T(8,128)S(1)} %get-tuple-element.6, f32[2,16,64]{2,1,0:T(8,128)S(1)} %get-tuple-element.7, f32[2,16,64]{2,1,0:T(8,128)S(1)} %get-tuple-element.5), kind=kLoop, calls=%fused_computation.2 | loop fusion | flops 4096 | bytes 28672 | tf_op jit(solution)/shard_map/transpose | solution.py:304

commit v3 on v1

--- a/solution.py
+++ b/solution.py
@@ -96,7 +96,7 @@
 
 
 def gather_and_solve(
-    sizes, pts_hbm, tgt_hbm, sol_ref, res_ref, pts, tgt, kmat, stage,
+    sizes, pts_hbm, tgt_hbm, base_ref, along_ref, alpha_ref, pts, tgt, kmat,
     local_sem, psend, precv, tsend, trecv,
 ):
     nz, nw, nx = sizes
@@ -242,22 +242,29 @@
     for step in range(ITERS):
         image = operate(direction)
         alpha = norm_now / over_points(direction * image)
-        solution = solution + alpha * direction
-        residual = residual - alpha * image
         if step + 1 < ITERS:
+            solution = solution + alpha * direction
+            residual = residual - alpha * image
             norm_next = over_points(residual * residual)
             direction = residual + (norm_next / norm_now) * direction
             norm_now = norm_next
-    own = z * nw + w
-    per = LANES // count
-    for index, (values, out) in enumerate(((solution, sol_ref), (residual, res_ref))):
-        for k in range(total // LANES):
-            stage[index, k] = values[:, k * LANES:(k + 1) * LANES]
-        piece = stage[index, own // per]
-        mine = piece[:, 0:count]
+
+    def mine(values):
+        per = LANES // count
+        own = z * nw + w
+        piece = values[:, 0:LANES]
+        for k in range(1, total // LANES):
+            piece = jnp.where(own // per == k, values[:, k * LANES:(k + 1) * LANES], piece)
+        part = piece[:, 0:count]
         for k in range(1, per):
-            mine = jnp.where(own % per == k, piece[:, k * count:(k + 1) * count], mine)
-        out[...] = mine
+            part = jnp.where(own % per == k, piece[:, k * count:(k + 1) * count], part)
+        return part
+
+    base_ref[0] = mine(solution)
+    base_ref[1] = mine(residual)
+    along_ref[0] = mine(direction)
+    along_ref[1] = mine(image)
+    alpha_ref[...] = jnp.broadcast_to(alpha, alpha_ref.shape)
     for copy in sends:
         copy.wait_send()
 
@@ -271,17 +278,19 @@
     ny = nw // CORES
     point_sends = (nz - 1) + nz * (ny * nx) + nz * (ny * nx - 1)
     target_sends = (nz - 1) + nz * ny + nz * (ny - 1)
-    out = jax.ShapeDtypeStruct((rhs, count), jnp.float32)
-    sol, res = pl.pallas_call(
+    base, along, alpha = pl.pallas_call(
         functools.partial(gather_and_solve, sizes),
-        out_shape=(out, out),
+        out_shape=(
+            pltpu.VMEM((2, rhs, count), jnp.float32),
+            pltpu.VMEM((2, rhs, count), jnp.float32),
+            pltpu.VMEM((rhs, count), jnp.float32),
+        ),
         in_specs=[pl.BlockSpec(memory_space=pl.ANY)] * 2,
-        out_specs=[pl.BlockSpec(memory_space=pltpu.VMEM)] * 2,
+        out_specs=[pl.BlockSpec(memory_space=pltpu.VMEM)] * 3,
         scratch_shapes=[
             pltpu.VMEM((total, width), jnp.bfloat16),
             pltpu.VMEM((groups, rhs, count), jnp.float32),
             pltpu.VMEM((total, total), jnp.bfloat16),
-            pltpu.VMEM((2, total // LANES, rhs, LANES), jnp.float32),
             pltpu.SemaphoreType.DMA((2,)),
             pltpu.SemaphoreType.DMA((point_sends,)),
             pltpu.SemaphoreType.DMA((nx, groups)),
@@ -290,7 +299,9 @@
         ],
         compiler_params=pltpu.CompilerParams(collective_id=0, has_side_effects=True),
     )(points, targets.T)
-    return sol.T, res.T
+    last = base[0] + alpha * along[0]
+    left = base[1] - alpha * along[1]
+    return last.T, left.T
 
 
 def solution(mesh):

time: 20.6 us -> 18.6 us (0.903)
  local copies, waits for them, and re-layouts: 1.9 us -> 0 us
  Pallas kernels: 17.8 us -> 17.1 us
  other arithmetic: 0 us -> 0.61 us
    unnamed x4 -> x0, local copies, waits for them, and re-layouts: 1.9 us -> none
    pallas_call x1, Pallas kernels: 17.8 us -> 17.1 us  [local_small(): pl.pallas_call(functools.partial(gather_and_solve, sizes), out_shape=(plt...]
    transpose x0 -> x1, other arithmetic: none -> 0.61 us  [local_small(): return (last.T, left.T)]
where the time goes in v3:
time: 18.6 us; the launch traced here: 18.4 us
  Pallas kernels  17.1 us (92%)
  between operations  0.64 us (3%)
  other arithmetic  0.61 us (3%)
    pallas_call x1, Pallas kernels, local_small(): pl.pallas_call(functools.partial(gather_and_solve, sizes), out_shape=(plt...  17.1 us
    transpose x1, other arithmetic, local_small(): return (last.T, left.T)  0.61 us

profile of v3, /device:TPU:1, one launch (start us, length us, event | category | flops | bytes accessed | tf_op | source)
XLA Modules:
  0.0 18.4 jit_solution(477295791223672676)
XLA Ops:
  0.6 17.1 %shard_map.41 = (f32[2,16,64]{2,1,0:T(8,128)S(1)}, f32[2,16,64]{2,1,0:T(8,128)S(1)}, f32[16,64]{1,0:T(8,128)S(1)}) custom-call(bf16[64,128]{1,0:T(8,128)(2,1)} %pts_hbm.1, f32[16,64]{1,0:T(8,128)} %bitcast.21), custom_call_target="tpu_custom_call" | custom-call | tf_op jit(solution)/shard_map/pallas_call | solution.py:281
  17.7 0.6 %fusion.1 = (f32[64,16]{0,1:T(8,128)}, f32[64,16]{0,1:T(8,128)}) fusion(f32[16,64]{1,0:T(8,128)S(1)} %get-tuple-element.6, f32[2,16,64]{2,1,0:T(8,128)S(1)} %get-tuple-element.7, f32[2,16,64]{2,1,0:T(8,128)S(1)} %get-tuple-element.5), kind=kLoop, calls=%fused_computation.2 | loop fusion | flops 4096 | bytes 28672 | tf_op jit(solution)/shard_map/transpose | solution.py:304

commit v4 on v3

--- a/solution.py
+++ b/solution.py
@@ -97,7 +97,7 @@
 
 def gather_and_solve(
     sizes, pts_hbm, tgt_hbm, base_ref, along_ref, alpha_ref, pts, tgt, kmat,
-    local_sem, psend, precv, tsend, trecv,
+    local_sem, send_sem, line_sem, plane_sem, side_sem, partner_sem,
 ):
     nz, nw, nx = sizes
     ny = nw // CORES
@@ -110,42 +110,34 @@
     def shift(value, by, size):
         return lax.rem(value + by, size)
 
-    sends = []
-
     def points_at(zb, wb, xb):
         rows = pl.ds(pl.multiple_of((zb * nw + wb) * count, count), count)
         return pts.at[rows, pl.ds(pl.multiple_of(xb * feats, feats), feats)]
 
-    def points_copy(block, to, slot):
+    def part(kind, block):
         zb, wb, xb = block
-        where = points_at(zb, wb, xb)
+        return points_at(zb, wb, xb) if kind == 0 else tgt.at[zb * nw + wb]
+
+    def make(kind, block, to, recv_sem):
+        where = part(kind, block)
         return pltpu.make_async_remote_copy(
-            src_ref=where, dst_ref=where, send_sem=psend.at[slot],
-            recv_sem=precv.at[xb, zb * nw + wb], device_id=to, device_id_type=MESH,
-        )
-
-    def targets_copy(block, to, slot):
-        zb, wb = block
-        where = tgt.at[zb * nw + wb]
-        return pltpu.make_async_remote_copy(
-            src_ref=where, dst_ref=where, send_sem=tsend.at[slot],
-            recv_sem=trecv.at[zb * nw + wb], device_id=to, device_id_type=MESH,
-        )
-
-    used = {"p": 0, "t": 0}
-
-    def send(kind, block, to):
-        make = points_copy if kind == "p" else targets_copy
-        copy = make(block, to, used[kind])
-        used[kind] += 1
-        copy.start()
-        sends.append(copy)
-
-    def arrived(kind, block):
-        make = points_copy if kind == "p" else targets_copy
-        make(block, (z, other, x), 0).wait_recv()
-
-    line = [(shift(z, d, nz), w, x) for d in range(1, nz)]
+            src_ref=where, dst_ref=where, send_sem=send_sem.at[kind],
+            recv_sem=recv_sem, device_id=to, device_id_type=MESH,
+        )
+
+    sent = [0, 0]
+
+    def send(kind, block, to, recv_sem):
+        make(kind, block, to, recv_sem).start()
+        sent[kind] += 1
+
+    def arrived(kind, block, recv_sem):
+        make(kind, block, (z, other, x), recv_sem).wait_recv()
+
+    def in_plane(kind, d, dy, dx):
+        return plane_sem.at[d, dy, dx] if kind == 0 else side_sem.at[d, dy]
+
+    line = [(d, (shift(z, d, nz), w, x)) for d in range(1, nz)]
     plane = [
         (dy, dx, (z, shift(y, dy, ny) * CORES + c, shift(x, dx, nx)))
         for dy in range(ny) for dx in range(nx) if dy or dx
@@ -157,45 +149,50 @@
     own_points.start()
     own_targets.start()
     barrier = pltpu.get_barrier_semaphore()
-    peers = line + [to for dy, dx, to in plane] + [partner]
+    peers = [to for d, to in line] + [to for dy, dx, to in plane] + [partner]
     for to in peers:
         pl.semaphore_signal(barrier, inc=1, device_id=to, device_id_type=MESH)
     own_points.wait()
     own_targets.wait()
     pl.semaphore_wait(barrier, len(peers))
 
-    def to_plane(zb):
-        for dy, dx, to in plane:
-            send("p", (zb, w, x), to)
-            if dx == 0:
-                send("t", (zb, w), to)
-        send("p", (zb, w, x), partner)
-        send("t", (zb, w), partner)
-
-    for to in line:
-        send("p", (z, w, x), to)
-        send("t", (z, w), to)
-    to_plane(z)
-    for d in range(1, nz):
-        zb = shift(z, d, nz)
-        arrived("p", (zb, w, x))
-        arrived("t", (zb, w))
-        to_plane(zb)
-    for d in range(nz):
+    def to_plane(d):
         zb = shift(z, d, nz)
         for dy, dx, to in plane:
-            arrived("p", (zb, to[1], to[2]))
-            send("p", (zb, to[1], to[2]), partner)
+            back_y, back_x = (ny - dy) % ny, (nx - dx) % nx
+            send(0, (zb, w, x), to, in_plane(0, d, back_y, back_x))
             if dx == 0:
-                arrived("t", (zb, to[1]))
-                send("t", (zb, to[1]), partner)
+                send(1, (zb, w, x), to, in_plane(1, d, back_y, back_x))
+        for kind in range(2):
+            send(kind, (zb, w, x), partner, partner_sem.at[kind])
+
+    for d, to in line:
+        for kind in range(2):
+            send(kind, (z, w, x), to, line_sem.at[kind, nz - d])
+    to_plane(0)
+    for d in range(1, nz):
+        for kind in range(2):
+            arrived(kind, (shift(z, d, nz), w, x), line_sem.at[kind, d])
+        to_plane(d)
     for d in range(nz):
-        zb = shift(z, d, nz)
-        for dy in range(ny):
-            wb = shift(y, dy, ny) * CORES + (1 - c)
-            for dx in range(nx):
-                arrived("p", (zb, wb, shift(x, dx, nx)))
-            arrived("t", (zb, wb))
+        for dy, dx, to in plane:
+            block = (shift(z, d, nz), to[1], to[2])
+            for kind in range(2 if dx == 0 else 1):
+                arrived(kind, block, in_plane(kind, d, dy, dx))
+                send(kind, block, partner, partner_sem.at[kind])
+
+    def all_of(kind, blocks):
+        return pts.at[0:blocks * count // nx] if kind == 0 else tgt.at[0:blocks]
+
+    def of_bytes(kind, blocks):
+        where = all_of(kind, blocks)
+        return pltpu.make_async_remote_copy(
+            src_ref=where, dst_ref=where, send_sem=send_sem.at[kind],
+            recv_sem=partner_sem.at[kind], device_id=partner, device_id_type=MESH,
+        )
+
+    of_bytes(0, nz * ny * nx).wait_recv()
+    of_bytes(1, nz * ny).wait_recv()
 
     total, width = pts.shape
     factor = math.log2(math.e) / (2.0 * width)
@@ -265,8 +262,8 @@
     along_ref[0] = mine(direction)
     along_ref[1] = mine(image)
     alpha_ref[...] = jnp.broadcast_to(alpha, alpha_ref.shape)
-    for copy in sends:
-        copy.wait_send()
+    for kind in range(2):
+        of_bytes(kind, sent[kind]).wait_send()
 
 
 def local_small(sizes, points, targets):
@@ -276,8 +273,6 @@
     total, width = nz * nw * count, nx * feats
     groups = nz * nw
     ny = nw // CORES
-    point_sends = (nz - 1) + nz * (ny * nx) + nz * (ny * nx - 1)
-    target_sends = (nz - 1) + nz * ny + nz * (ny - 1)
     base, along, alpha = pl.pallas_call(
         functools.partial(gather_and_solve, sizes),
         out_shape=(
@@ -292,10 +287,11 @@
             pltpu.VMEM((groups, rhs, count), jnp.float32),
             pltpu.VMEM((total, total), jnp.bfloat16),
             pltpu.SemaphoreType.DMA((2,)),
-            pltpu.SemaphoreType.DMA((point_sends,)),
-            pltpu.SemaphoreType.DMA((nx, groups)),
-            pltpu.SemaphoreType.DMA((target_sends,)),
-            pltpu.SemaphoreType.DMA((groups,)),
+            pltpu.SemaphoreType.DMA((2,)),
+            pltpu.SemaphoreType.DMA((2, nz)),
+            pltpu.SemaphoreType.DMA((nz, ny, nx)),
+            pltpu.SemaphoreType.DMA((nz, ny)),
+            pltpu.SemaphoreType.DMA((2,)),
         ],
         compiler_params=pltpu.CompilerParams(collective_id=0, has_side_effects=True),
     )(points, targets.T)

time: 18.6 us -> 18 us (0.968)
  Pallas kernels: 17.1 us -> 16.5 us
    pallas_call x1, Pallas kernels: 17.1 us -> 16.5 us  [local_small(): pl.pallas_call(functools.partial(gather_and_solve, sizes), out_shape=(plt...]
where the time goes in v4:
time: 18 us; the launch traced here: 17.8 us
  Pallas kernels  16.5 us (92%)
  between operations  0.64 us (4%)
  other arithmetic  0.61 us (3%)
    pallas_call x1, Pallas kernels, local_small(): pl.pallas_call(functools.partial(gather_and_solve, sizes), out_shape=(plt...  16.5 us
    transpose x1, other arithmetic, local_small(): return (last.T, left.T)  0.61 us

profile of v4, /device:TPU:1, one launch (start us, length us, event | category | flops | bytes accessed | tf_op | source)
XLA Modules:
  0.0 17.8 jit_solution(3045514413410174114)
XLA Ops:
  0.6 16.5 %shard_map.41 = (f32[2,16,64]{2,1,0:T(8,128)S(1)}, f32[2,16,64]{2,1,0:T(8,128)S(1)}, f32[16,64]{1,0:T(8,128)S(1)}) custom-call(bf16[64,128]{1,0:T(8,128)(2,1)} %pts_hbm.1, f32[16,64]{1,0:T(8,128)} %bitcast.21), custom_call_target="tpu_custom_call" | custom-call | tf_op jit(solution)/shard_map/pallas_call | solution.py:276
  17.2 0.6 %fusion.1 = (f32[64,16]{0,1:T(8,128)}, f32[64,16]{0,1:T(8,128)}) fusion(f32[16,64]{1,0:T(8,128)S(1)} %get-tuple-element.6, f32[2,16,64]{2,1,0:T(8,128)S(1)} %get-tuple-element.7, f32[2,16,64]{2,1,0:T(8,128)S(1)} %get-tuple-element.5), kind=kLoop, calls=%fused_computation.2 | loop fusion | flops 4096 | bytes 28672 | tf_op jit(solution)/shard_map/transpose | solution.py:300
